TPU v7x, 256 devices: a whole 4x4x8 slice. The times are simulated.
256 devices in a mesh: row: 32 (over y, x, core), col: 8 (over z).
Axes of the slice: x: 4, y: 4, z: 8, core: 2. Of those that a mesh axis runs over, the one named last changes fastest.
Arguments:
- features: bfloat16 [262144, 256], P(('col', 'row')), may hold values from -6 to 6
- block_values: bfloat16 [32, 8, 192, 128, 128], P('row', 'col'), may hold values from -0.1875 to 0.1875
- row_ptr: int32 [32, 8, 65], P('row', 'col'), may hold values from 0 to 144, as said below
- block_cols: int32 [32, 8, 192], P('row', 'col'), may hold values from 0 to 2047, as said below
Outputs:
- product: bfloat16 [262144, 256], P(('row', 'col'))
Inputs may be any that keep to these rules, and one draw needn't show every extreme that they name: row_ptr[r, c, 0] = 0, row_ptr never falls along its last dimension, row_ptr[r, c, 64] <= 144, and on exactly one device row_ptr[r, c, 64] = 144. block_cols[r, c, s] lies in c * 256 to (c + 1) * 256 - 1; a block column may repeat within a block row, and repeated blocks add.
All inputs are finite; a program needn't handle non-finite values.
Results may differ from a plain program's by a relative error of at most 0.001.
Values may be sent and summed in bfloat16 or wider, within the bound.
A program may use at most 128 MiB of HBM per device.

v0:
```python
import jax
import jax.numpy as jnp
from jax import lax
from jax.sharding import PartitionSpec as P


def row_weights(pointers, slot_count):
    slot_ids = jnp.arange(slot_count, dtype=jnp.int32)
    inside = (pointers[:-1, None] <= slot_ids[None, :]) & (slot_ids[None, :] < pointers[1:, None])
    return inside.astype(jnp.float32)


def local(features, block_values, row_ptr, block_cols):
    values = block_values[0, 0]
    pointers = row_ptr[0, 0]
    slot_count = values.shape[0]
    block_size = values.shape[1]
    local_rows = pointers.shape[0] - 1
    group_blocks = features.shape[0] * lax.axis_size("row") // block_size
    columns = block_cols[0, 0] - lax.axis_index("col") * group_blocks
    weights = row_weights(pointers, slot_count)
    panel = lax.all_gather(features, "row", axis=0, tiled=True)
    panel_blocks = panel.reshape(group_blocks, block_size, panel.shape[1])
    blocks = panel_blocks[columns]
    panel_width = blocks.shape[2]
    products = jnp.einsum("sij,sjk->sik", values, blocks, preferred_element_type=jnp.float32)
    summed = jnp.einsum("rs,sik->rik", weights, products, precision=lax.Precision.HIGHEST)
    partial_value = summed.reshape(local_rows * block_size, panel_width)
    return lax.psum_scatter(partial_value, "col", scatter_dimension=0, tiled=True).astype(
        jnp.bfloat16
    )


def solution(mesh):
    return jax.shard_map(
        local,
        mesh=mesh,
        in_specs=(
            P(("col", "row"), None),
            P("row", "col", None, None, None),
            P("row", "col", None),
            P("row", "col", None),
        ),
        out_specs=P(("row", "col"), None),
        check_vma=False,
    )
```

profile of v0, /device:TPU:1, one launch (start us, length us, event | category | flops | bytes accessed | tf_op | source)
XLA Modules:
  0.0 271.3 jit_solution(18288840920602254355)
XLA Ops:
  6.5 0.0 all-gather.2.cloned.1.call-start
  6.5 0.7 all-gather.2.cloned.1.call-update
  7.3 0.0 reduce-scatter.2.cloned.1.call-start
  7.3 0.7 compare_select_fusion
  8.0 0.8 slice_bitcast_fusion.1
  8.8 82.9 %all-gather.2.cloned.1.call-done = bf16[32768,256]{1,0:T(8,128)(2,1)} async-done(((bf16[1024,256]{1,0:T(8,128)(2,1)}), bf16[32768,256]{1,0:T(8,128)(2,1)}) %all-gather.2.cloned.1.call-update) | async-done | bytes 16777232 | tf_op jit(solution)/shard_map/all_gather | solution.py:22
  91.7 14.1 %gather_fusion = bf16[192,128,256]{2,1,0:T(8,128)(2,1)} fusion(bf16[256,128,256]{2,1,0:T(8,128)(2,1)} %bitcast.20, s32[1024]{0:T(1024)S(1)} %pad_clamp_fusion), kind=kCustom, calls=%fused_computation | custom fusion | bytes 25166592 | tf_op jit(solution)/shard_map/gather | solution.py:24
  105.7 13.8 %fusion.2 = f32[192,256,128]{2,1,0:T(8,128)} fusion(bf16[192,128,256]{2,1,0:T(8,128)(2,1)} %gather_fusion, bf16[1,1,192,128,128]{4,3,2,1,0:T(8,128)(2,1)} %param.5), kind=kOutput, calls=%fused_computation.3 | convolution fusion | flops 1610612736 | bytes 44040192 | tf_op jit(solution)/shard_map/sij,sjk->sik/dot_general | solution.py:26
  119.5 24.9 %copy.6 = f32[192,256,128]{1,0,2:T(8,128)} copy(f32[192,256,128]{2,1,0:T(8,128)} %fusion.2) | data formatting | bytes 50331648 | tf_op jit(solution)/shard_map/sij,sjk->sik/dot_general | solution.py:26
  144.4 15.7 %fusion = f32[64,128,256]{2,0,1:T(8,128)S(1)} fusion(f32[192,256,128]{1,0,2:T(8,128)} %copy.6, s32[64]{0:T(128)S(1)} %get-tuple-element.6, s32[64]{0:T(128)S(1)} %get-tuple-element.5), kind=kOutput, calls=%fused_computation.1 | convolution fusion | flops 4831875072 | bytes 33554944 | tf_op jit(solution)/shard_map/rs,sik->rik/dot_general | solution.py:27
  160.1 8.1 %copy.5 = f32[64,128,256]{2,1,0:T(8,128)} copy(f32[64,128,256]{2,0,1:T(8,128)S(1)} %fusion) | data formatting | bytes 16777216 | tf_op jit(solution)/shard_map/rs,sik->rik/dot_general | solution.py:27
  168.2 0.0 reduce-scatter.2.cloned.1.call-update
  168.2 94.2 %reduce-scatter.2.cloned.1.call-done = f32[1024,256]{1,0:T(8,128)} async-done(((f32[8192,256]{1,0:T(8,128)}), f32[1024,256]{1,0:T(8,128)}) %reduce-scatter.2.cloned.1.call-update) | async-done | bytes 1048592 | tf_op jit(solution)/shard_map/reduce_scatter | solution.py:29
  262.4 2.1 convert_element_type.4
  (1 shorter events, 0.0 us)
Async XLA Ops:
  6.5 85.1 %all-gather.2.cloned.1.call-start = ((), (), s32[]{:S(2)}) async-start(), calls=%async_computation.1 | async-start | bytes 17301504 | tf_op jit(solution)/shard_map/all_gather | solution.py:22
  7.3 255.1 %reduce-scatter.2.cloned.1.call-start = ((), (), s32[]{:S(2)}) async-start(), calls=%async_computation.2 | async-start | bytes 9437184 | tf_op jit(solution)/shard_map/reduce_scatter | solution.py:29
Sparse Core Ops, SparseCore 0:
  9.9 81.7 all-gather.1
  168.3 94.0 reduce-scatter.1
where the time goes:
time: 272 us; the launch traced here: 271 us
  waiting for transfers between devices  178 us (65%)
  local copies, waits for them, and re-layouts  47.8 us (18%)
  matrix products  29.5 us (11%)
  between operations  13.4 us (5%)
  other arithmetic  2.76 us (1%)
    reduce_scatter x1, waiting for transfers between devices, local(): lax.psum_scatter(partial_value, 'col', scatter_dimension=0, tiled=True)  94.2 us
    all_gather x1, waiting for transfers between devices, local(): panel = lax.all_gather(features, 'row', axis=0, tiled=True)  82.9 us
    dot_general x1, local copies, waits for them, and re-layouts, local(): jnp.einsum('sij,sjk->sik', values, blocks, preferred_element_type=jnp.flo...  24.9 us
    dot_general x1, matrix products, local(): jnp.einsum('rs,sik->rik', weights, products, precision=lax.Precision.HIGH...  15.7 us
    gather x1, local copies, waits for them, and re-layouts, local(): blocks = panel_blocks[columns]  14.1 us
    dot_general x1, matrix products, local(): jnp.einsum('sij,sjk->sik', values, blocks, preferred_element_type=jnp.flo...  13.8 us
    dot_general x1, local copies, waits for them, and re-layouts, local(): jnp.einsum('rs,sik->rik', weights, products, precision=lax.Precision.HIGH...  8.07 us
  transfers between devices with their start and end apart: 2, of which 2 were waited for; matrix products, arithmetic and copies ran while one was open for 1% of the time, Pallas kernels for 0%

commit v1 on v0

v1 whole, which is shorter than its diff:
```python
import functools

import jax
import jax.numpy as jnp
from jax import lax
from jax.experimental import pallas as pl
from jax.experimental.pallas import tpu as pltpu
from jax.sharding import PartitionSpec as P

MESH = pl.DeviceIdType.MESH
SIDE = 4
GROUP = 8
ROOM = 144
LIMIT = 32767.0


def gather_kernel(x_ref, out_ref, own, local_sem, send_sem, recv_sem, near_send, near_recv):
    me, col = lax.axis_index("row"), lax.axis_index("col")
    core, x, y = lax.rem(me, 2), lax.rem(me // 2, SIDE), me // (2 * SIDE)
    depth = own.shape[0]
    half, quarter = depth // 2, depth // 4
    sends, slots, near = [], {}, []

    def rank(h, i, j, which):
        dx, dy = (i, j) if h == 0 else (j, i)
        return (lax.rem(y + dy + SIDE, SIDE) * SIDE + lax.rem(x + dx + SIDE, SIDE)) * 2 + which

    def rows(h, part):
        return {
            "all": pl.ds(h * half, half),
            "first": pl.ds(h * half, quarter),
            "second": pl.ds(h * half + quarter, quarter),
        }[part]

    def key(h, i, j, part):
        return (h, (i + 1) % SIDE, (j + 1) % SIDE, part)

    def send(h, i, j, part, di, dj):
        span = rows(h, part)
        dst = out_ref.at[rank(h, i, j, core), span]
        src = own.at[span] if (i, j) == (0, 0) else dst
        k = len(sends)
        copy = pltpu.make_async_remote_copy(
            src_ref=src,
            dst_ref=dst,
            send_sem=send_sem.at[k],
            recv_sem=recv_sem.at[k],
            device_id=(rank(h, di, dj, core), col),
            device_id_type=MESH,
        )
        copy.start()
        sends.append(copy)
        slots[key(h, i - di, j - dj, part)] = k

    def arrive(h, i, j, part):
        k = slots[key(h, i, j, part)]
        span = out_ref.at[rank(h, i, j, core), rows(h, part)]
        pltpu.make_async_remote_copy(
            src_ref=span,
            dst_ref=span,
            send_sem=send_sem.at[k],
            recv_sem=recv_sem.at[k],
            device_id=(me, col),
            device_id_type=MESH,
        ).wait_recv()

    def across(src, dst, other):
        k = len(near)
        copy = pltpu.make_async_remote_copy(
            src_ref=src,
            dst_ref=dst,
            send_sem=near_send.at[k],
            recv_sem=near_recv.at[k],
            device_id=(me + 1 - 2 * core, col),
            device_id_type=MESH,
        )
        copy.start()
        near.append((copy, other))

    def hand_on(h, i, j):
        span = rows(h, "all")
        here = out_ref.at[rank(h, i, j, core), span]
        across(here, here, out_ref.at[rank(h, i, j, 1 - core), span])

    load = pltpu.make_async_copy(x_ref, own, local_sem.at[0])
    load.start()
    barrier = pltpu.get_barrier_semaphore()
    neighbours = [rank(0, 1, 0, core), rank(0, -1, 0, core), rank(0, 0, 1, core), rank(0, 0, -1, core), rank(0, 0, 0, 1 - core)]
    for device in neighbours:
        pl.semaphore_signal(barrier, inc=1, device_id=(device, col), device_id_type=MESH)
    pl.semaphore_wait(barrier, len(neighbours))
    load.wait()

    for h in (0, 1):
        for s in (1, -1):
            send(h, 0, 0, "all", s, 0)
    for h in (0, 1):
        for s in (1, -1):
            send(h, 0, 0, "all", 0, s)
    across(own, out_ref.at[me], out_ref.at[me + 1 - 2 * core])
    keep = pltpu.make_async_copy(own, out_ref.at[me], local_sem.at[1])
    keep.start()
    part_of = {-1: "first", 1: "second"}
    for s in (-1, 1):
        for h in (0, 1):
            arrive(h, s, 0, "all")
            send(h, s, 0, part_of[s], -s, 0)
            send(h, s, 0, "all", 0, 1)
            send(h, s, 0, "all", 0, -1)
            hand_on(h, s, 0)
    for s in (-1, 1):
        for h in (0, 1):
            arrive(h, 0, s, "all")
            send(h, 0, s, part_of[s], 0, -s)
            hand_on(h, 0, s)
    for h in (0, 1):
        for part in ("first", "second"):
            arrive(h, 2, 0, part)
        send(h, 2, 0, "all", 0, 1)
        send(h, 2, 0, "all", 0, -1)
        hand_on(h, 2, 0)
    for i in (-1, 1, 2):
        for s in (-1, 1):
            for h in (0, 1):
                arrive(h, i, s, "all")
                send(h, i, s, part_of[s], 0, -s)
                hand_on(h, i, s)
    for i in (0, -1, 1, 2):
        for h in (0, 1):
            for part in ("first", "second"):
                arrive(h, i, 2, part)
            hand_on(h, i, 2)
    keep.wait()
    for k, (copy, other) in enumerate(near):
        pltpu.make_async_remote_copy(
            src_ref=other,
            dst_ref=other,
            send_sem=near_send.at[k],
            recv_sem=near_recv.at[k],
            device_id=(me + 1 - 2 * core, col),
            device_id_type=MESH,
        ).wait_recv()
    for copy, _ in near:
        copy.wait_send()
    for copy in sends:
        copy.wait_send()


def gather(features, ranks):
    depth, width = features.shape
    links, crossings = 40, 31
    return pl.pallas_call(
        gather_kernel,
        out_shape=jax.ShapeDtypeStruct((ranks, depth, width), features.dtype),
        in_specs=[pl.BlockSpec(memory_space=pl.ANY)],
        out_specs=pl.BlockSpec(memory_space=pl.ANY),
        scratch_shapes=[
            pltpu.VMEM((depth, width), features.dtype),
            pltpu.SemaphoreType.DMA((2,)),
            pltpu.SemaphoreType.DMA((links,)),
            pltpu.SemaphoreType.DMA((links,)),
            pltpu.SemaphoreType.DMA((crossings,)),
            pltpu.SemaphoreType.DMA((crossings,)),
        ],
        compiler_params=pltpu.CompilerParams(collective_id=0, has_side_effects=True),
        name="gather",
    )(features)


def multiply_kernel(ptr_ref, cols_ref, x_ref, a_ref, p_ref, xbuf, abuf, row_of, xsem, asem):
    blocks, side = x_ref.shape[0], x_ref.shape[1]
    local_rows = ptr_ref.shape[0] - 1
    used = ptr_ref[local_rows]
    groups = (used + GROUP - 1) // GROUP

    def values(g):
        span = pl.ds(g * GROUP, GROUP)
        return pltpu.make_async_copy(a_ref.at[span], abuf.at[span], asem.at[g])

    def fetch(g, carry):
        values(g).start()
        for u in range(GROUP):
            s = g * GROUP + u
            pltpu.make_async_copy(x_ref.at[lax.rem(cols_ref[s], blocks)], xbuf.at[s], xsem.at[g]).start()
        return carry

    lax.fori_loop(0, groups, fetch, 0)

    def clear(i, carry):
        p_ref[pl.ds(pl.multiple_of(i * side, side), side), :] = jnp.zeros((side, p_ref.shape[1]), jnp.float32)
        return carry

    lax.fori_loop(0, local_rows, clear, 0)

    def label(i, carry):
        def one(s, c):
            row_of[s] = i
            return c

        return lax.fori_loop(ptr_ref[i], ptr_ref[i + 1], one, carry)

    lax.fori_loop(0, local_rows, label, 0)

    def spare(s, c):
        row_of[s] = local_rows
        return c

    lax.fori_loop(used, groups * GROUP, spare, 0)

    def step(g, carry):
        values(g).wait()
        span = pl.ds(g * GROUP, GROUP)
        pltpu.make_async_copy(x_ref.at[pl.ds(0, GROUP)], xbuf.at[span], xsem.at[g]).wait()
        for u in range(GROUP):
            s = g * GROUP + u
            product = jnp.dot(abuf[s], xbuf[s], preferred_element_type=jnp.float32)
            place = pl.ds(pl.multiple_of(row_of[s] * side, side), side)
            p_ref[place, :] += product
        return carry

    lax.fori_loop(0, groups, step, 0)


def multiply(pointers, columns, panel, values):
    side, width = panel.shape[1], panel.shape[2]
    local_rows = pointers.shape[0] - 1
    return pl.pallas_call(
        multiply_kernel,
        out_shape=jax.ShapeDtypeStruct(((local_rows + 1) * side, width), jnp.float32),
        in_specs=[
            pl.BlockSpec(memory_space=pltpu.SMEM),
            pl.BlockSpec(memory_space=pltpu.SMEM),
            pl.BlockSpec(memory_space=pl.ANY),
            pl.BlockSpec(memory_space=pl.ANY),
        ],
        out_specs=pl.BlockSpec(memory_space=pltpu.VMEM),
        scratch_shapes=[
            pltpu.VMEM((ROOM, side, width), jnp.bfloat16),
            pltpu.VMEM((ROOM, side, side), jnp.bfloat16),
            pltpu.SMEM((ROOM,), jnp.int32),
            pltpu.SemaphoreType.DMA((ROOM // GROUP,)),
            pltpu.SemaphoreType.DMA((ROOM // GROUP,)),
        ],
        compiler_params=pltpu.CompilerParams(vmem_limit_bytes=30 * 1024 * 1024),
        name="multiply",
    )(pointers, columns, panel, values)


def reduce_kernel(
    side, p_ref, o_ref, part, sent, got, sent_scale, got_scale, load_sem, send_sem, recv_sem, scale_send, scale_recv
):
    row, me = lax.axis_index("row"), lax.axis_index("col")
    ring = lax.axis_size("col")
    depth, width = o_ref.shape
    lanes = width // 2
    far = ring // 2

    def at(offset):
        return lax.rem(me + offset + ring, ring)

    order = [far] + [s * t for t in range(far - 1, 0, -1) for s in (1, -1)] + [0]
    place = {offset: n for n, offset in enumerate(order)}
    place[-far] = place[far]
    loads = {}
    for n, offset in enumerate(order):
        loads[n] = pltpu.make_async_copy(
            p_ref.at[pl.ds(pl.multiple_of(at(offset) * depth, depth), depth)], part.at[n], load_sem.at[n]
        )
        loads[n].start()

    barrier = pltpu.get_barrier_semaphore()
    for s in (1, -1):
        pl.semaphore_signal(barrier, inc=1, device_id=(row, at(s)), device_id_type=MESH)
    pl.semaphore_wait(barrier, 2)

    def copies(w, k, s):
        return [
            pltpu.make_async_remote_copy(
                src_ref=a.at[w, k],
                dst_ref=b.at[w, k],
                send_sem=c.at[w, k],
                recv_sem=d.at[w, k],
                device_id=(row, at(s)),
                device_id_type=MESH,
            )
            for a, b, c, d in ((sent, got, send_sem, recv_sem), (sent_scale, got_scale, scale_send, scale_recv))
        ]

    def spread(w, k, j):
        return got[w, k, pl.ds(pl.multiple_of(j * side, side), side), :].astype(jnp.int32).astype(jnp.float32) * got_scale[
            w, k, pl.ds(j, 1), :
        ]

    def columns(w, k):
        h = w if k % 2 == 0 else 1 - w
        return pl.ds(h * lanes, lanes)

    loaded = set()

    def need(n):
        if n not in loaded:
            loaded.add(n)
            loads[n].wait()

    started = []
    for k in range(ring - 1):
        for w, s in ((0, 1), (1, -1)):
            n = place[s * (far - (k + 1) // 2)]
            need(n)
            if k >= 2:
                for copy in copies(w, k - 2, s):
                    copy.wait_recv()

            def code(j, carry, w=w, k=k, n=n):
                span = pl.ds(pl.multiple_of(j * side, side), side)
                value = part[n, span, columns(w, k)]
                if k >= 2:
                    value = value + spread(w, k - 2, j)
                top = jnp.maximum(jnp.max(jnp.abs(value), axis=0, keepdims=True), 1e-30)
                sent_scale[w, k, pl.ds(j, 1), :] = top * (1.0 / LIMIT)
                sent[w, k, span, :] = jnp.round(value * (LIMIT / top)).astype(jnp.int32).astype(jnp.int16)
                return carry

            lax.fori_loop(0, depth // side, code, 0)
            for copy in copies(w, k, s):
                copy.start()
                started.append(copy)

    need(place[0])
    for w, s in ((0, 1), (1, -1)):
        for k in (ring - 3, ring - 2):
            for copy in copies(w, k, s):
                copy.wait_recv()

    def finish(j, carry):
        span = pl.ds(pl.multiple_of(j * side, side), side)
        for h in (0, 1):
            cut = pl.ds(h * lanes, lanes)
            value = part[place[0], span, cut] + (spread(h, ring - 2, j) + spread(1 - h, ring - 3, j))
            o_ref[span, cut] = value.astype(o_ref.dtype)
        return carry

    lax.fori_loop(0, depth // side, finish, 0)
    for copy in started:
        copy.wait_send()


def reduce(partial_value, side, ring, depth):
    width = partial_value.shape[1]
    steps = ring - 1
    return pl.pallas_call(
        functools.partial(reduce_kernel, side),
        out_shape=jax.ShapeDtypeStruct((depth, width), jnp.bfloat16),
        in_specs=[pl.BlockSpec(memory_space=pl.ANY)],
        out_specs=pl.BlockSpec(memory_space=pltpu.VMEM),
        scratch_shapes=[
            pltpu.VMEM((ring, depth, width), jnp.float32),
            pltpu.VMEM((2, steps, depth, width // 2), jnp.int16),
            pltpu.VMEM((2, steps, depth, width // 2), jnp.int16),
            pltpu.VMEM((2, steps, depth // side, width // 2), jnp.float32),
            pltpu.VMEM((2, steps, depth // side, width // 2), jnp.float32),
            pltpu.SemaphoreType.DMA((ring,)),
            pltpu.SemaphoreType.DMA((2, steps)),
            pltpu.SemaphoreType.DMA((2, steps)),
            pltpu.SemaphoreType.DMA((2, steps)),
            pltpu.SemaphoreType.DMA((2, steps)),
        ],
        compiler_params=pltpu.CompilerParams(
            collective_id=1, has_side_effects=True, vmem_limit_bytes=20 * 1024 * 1024
        ),
        name="reduce",
    )(partial_value)


def local(features, block_values, row_ptr, block_cols):
    values, pointers, columns = block_values[0, 0], row_ptr[0, 0], block_cols[0, 0]
    side = values.shape[1]
    ranks, ring = lax.axis_size("row"), lax.axis_size("col")
    panel = gather(features, ranks)
    panel = panel.reshape(ranks * features.shape[0] // side, side, features.shape[1])
    partial_value = multiply(pointers, columns, panel, values)
    return reduce(partial_value, side, ring, (pointers.shape[0] - 1) * side // ring)


def solution(mesh):
    return jax.shard_map(
        local,
        mesh=mesh,
        in_specs=(
            P(("col", "row"), None),
            P("row", "col", None, None, None),
            P("row", "col", None),
            P("row", "col", None),
        ),
        out_specs=P(("row", "col"), None),
        check_vma=False,
    )
```

time: 272 us -> 110 us (0.40)
  waiting for transfers between devices: 178 us -> 0 us
  Pallas kernels: 0 us -> 106 us
  local copies, waits for them, and re-layouts: 47.8 us -> 3.58 us
  matrix products: 29.5 us -> 0 us
  between operations: 13.4 us -> 0.05 us
  other arithmetic: 2.76 us -> 0 us
    pallas_call x0 -> x3, Pallas kernels: none -> 106 us  [the longest x1 53.1 us: gather(): pl.pallas_call(gather_kernel, out_shape=jax.ShapeDtypeStruct((ranks, dept...]
    reduce_scatter x1 -> x0, waiting for transfers between devices: 94.2 us -> none  [local(): lax.psum_scatter(partial_value, 'col', scatter_dimension=0, tiled=True)]
    all_gather x1 -> x0, waiting for transfers between devices: 82.9 us -> none  [local(): panel = lax.all_gather(features, 'row', axis=0, tiled=True)]
    dot_general x2 -> x0, local copies, waits for them, and re-layouts: 33 us -> none  [the longest x1 24.9 us: local(): jnp.einsum('sij,sjk->sik', values, blocks, preferred_element_type=jnp.flo...]
    dot_general x2 -> x0, matrix products: 29.5 us -> none  [the longest x1 15.7 us: local(): jnp.einsum('rs,sik->rik', weights, products, precision=lax.Precision.HIGH...]
    gather x1 -> x0, local copies, waits for them, and re-layouts: 14.1 us -> none  [local(): blocks = panel_blocks[columns]]
    unnamed x0 -> x7, local copies, waits for them, and re-layouts: none -> 3.58 us
  transfers between devices with their start and end apart: 2 -> 0, of which waited for: 2 -> 0; matrix products, arithmetic and copies ran while one was open for 1% -> 0% of each run, Pallas kernels for 0% -> 0%
where the time goes in v1:
time: 110 us
  Pallas kernels  106 us (96%)
  local copies, waits for them, and re-layouts  3.58 us (3%)
    pallas_call x1, Pallas kernels, gather(): pl.pallas_call(gather_kernel, out_shape=jax.ShapeDtypeStruct((ranks, dept...  53.1 us
    pallas_call x1, Pallas kernels, reduce(): pl.pallas_call(functools.partial(reduce_kernel, side), out_shape=jax.Shap...  47.7 us
    pallas_call x1, Pallas kernels, multiply(): pl.pallas_call(multiply_kernel, out_shape=jax.ShapeDtypeStruct(((local_ro...  5.46 us
    unnamed x7, local copies, waits for them, and re-layouts  3.58 us

profile of v1, /device:TPU:1, one launch (start us, length us, event | category | flops | bytes accessed | tf_op | source)
XLA Modules:
  0.0 109.8 jit_solution(1153189718890034555)
XLA Ops:
  0.0 0.0 copy-start.1
  0.0 0.0 copy-start.2
  0.0 53.1 %gather.1 = bf16[32,1024,256]{2,1,0:T(8,128)(2,1)} custom-call(bf16[1024,256]{1,0:T(8,128)(2,1)} %x_ref.1), custom_call_target="tpu_custom_call" | custom-call | tf_op jit(solution)/shard_map/gather/pallas_call | solution.py:152
  53.1 0.0 copy-done.1
  53.1 0.0 copy-done.2
  53.1 0.0 copy-start
  53.1 2.8 %copy-done = bf16[1,1,192,128,128]{4,3,2,1,0:T(8,128)(2,1)S(1)} copy-done((bf16[1,1,192,128,128]{4,3,2,1,0:T(8,128)(2,1)S(1)}, bf16[1,1,192,128,128]{4,3,2,1,0:T(8,128)(2,1)}, u32[]{:S(2)}) %copy-start) | copy-done | bytes 6291480
  55.9 5.5 %multiply.1.p_ref = f32[8320,256]{1,0:T(8,128)S(1)} custom-call(s32[65]{0:T(128)S(1)} %bitcast.6, s32[192]{0:T(256)S(1)} %bitcast.5, bf16[256,128,256]{2,1,0:T(8,128)(2,1)} %bitcast.7, bf16[192,128,128]{2,1,0:T(8,128)(2,1)S(1)} %bitcast.4), custom_call_target="tpu_custom_call" | custom-call | tf_op jit(solution)/shard_map/multiply/pallas_call | solution.py:227
  61.3 47.7 %reduce.1 = bf16[1024,256]{1,0:T(8,128)(2,1)S(1)} custom-call(f32[8320,256]{1,0:T(8,128)S(1)} %multiply.1.p_ref), custom_call_target="tpu_custom_call" | custom-call | tf_op jit(solution)/shard_map/reduce/pallas_call | solution.py:351
  109.0 0.8 copy.6
Async XLA Ops:
  0.0 53.1 %copy-start.1 = (s32[1,1,192]{2,1,0:T(1,128)S(1)}, s32[1,1,192]{2,1,0:T(1,128)}, u32[]{:S(2)}) copy-start(s32[1,1,192]{2,1,0:T(1,128)} %param.7) | copy-start | bytes 2308
  0.0 53.1 %copy-start.2 = (s32[1,1,65]{2,1,0:T(1,128)S(1)}, s32[1,1,65]{2,1,0:T(1,128)}, u32[]{:S(2)}) copy-start(s32[1,1,65]{2,1,0:T(1,128)} %param.6) | copy-start | bytes 784
  53.1 2.8 %copy-start = (bf16[1,1,192,128,128]{4,3,2,1,0:T(8,128)(2,1)S(1)}, bf16[1,1,192,128,128]{4,3,2,1,0:T(8,128)(2,1)}, u32[]{:S(2)}) copy-start(bf16[1,1,192,128,128]{4,3,2,1,0:T(8,128)(2,1)} %param.5) | copy-start | bytes 18874372

commit v2 on v0

v2 whole, which is shorter than its diff:
```python
import jax
import jax.numpy as jnp
from jax import lax
from jax.experimental import pallas as pl
from jax.experimental.pallas import tpu as pltpu
from jax.sharding import PartitionSpec as P

MESH = pl.DeviceIdType.MESH
SIDE = 4
GROUP = 8
ROOM = 144
LIMIT = 32767.0
LINKS, CROSSINGS = 40, 31


class Gather:
    def __init__(self, c, panels, send_sem, recv_sem, near_send, near_recv):
        me, self.col = lax.axis_index("row"), lax.axis_index("col")
        self.c, self.panel = c, panels[c]
        self.core, self.x, self.y = lax.rem(me, 2), lax.rem(me // 2, SIDE), me // (2 * SIDE)
        self.depth = self.panel.shape[0] // lax.axis_size("row")
        self.send_sem, self.recv_sem, self.near_send, self.near_recv = send_sem, recv_sem, near_send, near_recv
        self.sends, self.slots, self.near = [], {}, []

    def rank(self, h, i, j, other=False):
        dx, dy = (i, j) if h == 0 else (j, i)
        core = 1 - self.core if other else self.core
        return (lax.rem(self.y + dy + SIDE, SIDE) * SIDE + lax.rem(self.x + dx + SIDE, SIDE)) * 2 + core

    def piece(self, h, i, j, part, other=False):
        half, quarter = self.depth // 2, self.depth // 4
        first, size = {"all": (0, half), "first": (0, quarter), "second": (quarter, quarter)}[part]
        return self.panel.at[pl.ds(self.rank(h, i, j, other) * self.depth + h * half + first, size)]

    def key(self, h, i, j, part):
        return (h, (i + 1) % SIDE, (j + 1) % SIDE, part)

    def link(self, k, ref, device):
        return pltpu.make_async_remote_copy(
            src_ref=ref,
            dst_ref=ref,
            send_sem=self.send_sem.at[self.c, k],
            recv_sem=self.recv_sem.at[self.c, k],
            device_id=(device, self.col),
            device_id_type=MESH,
        )

    def across(self, k, ref):
        return pltpu.make_async_remote_copy(
            src_ref=ref,
            dst_ref=ref,
            send_sem=self.near_send.at[self.c, k],
            recv_sem=self.near_recv.at[self.c, k],
            device_id=(self.rank(0, 0, 0, True), self.col),
            device_id_type=MESH,
        )

    def send(self, h, i, j, part, di, dj):
        k = len(self.sends)
        copy = self.link(k, self.piece(h, i, j, part), self.rank(h, di, dj))
        copy.start()
        self.sends.append(copy)
        self.slots[self.key(h, i - di, j - dj, part)] = k

    def arrive(self, h, i, j, part):
        self.link(self.slots[self.key(h, i, j, part)], self.piece(h, i, j, part), self.rank(h, 1, 0)).wait_recv()

    def hand_on(self, h, i, j):
        k = len(self.near)
        copy = self.across(k, self.piece(h, i, j, "all"))
        copy.start()
        self.near.append((copy, self.across(k, self.piece(h, i, j, "all", True))))

    def own(self):
        for di, dj in ((1, 0), (-1, 0), (0, 1), (0, -1)):
            for h in (0, 1):
                self.send(h, 0, 0, "all", di, dj)
        k = len(self.near)
        refs = [self.panel.at[pl.ds(self.rank(0, 0, 0, o) * self.depth, self.depth)] for o in (False, True)]
        copy = self.across(k, refs[0])
        copy.start()
        self.near.append((copy, self.across(k, refs[1])))

    def forward(self, h, i, j):
        self.send(h, i, j, "first" if j == -1 else "second", 0, -j)

    def first_hop(self):
        for s in (-1, 1):
            for h in (0, 1):
                self.arrive(h, s, 0, "all")
                self.send(h, s, 0, "first" if s == -1 else "second", -s, 0)
                self.send(h, s, 0, "all", 0, 1)
                self.send(h, s, 0, "all", 0, -1)
                self.hand_on(h, s, 0)

    def second_hop(self):
        for h in (0, 1):
            for part in ("first", "second"):
                self.arrive(h, 2, 0, part)
            self.send(h, 2, 0, "all", 0, 1)
            self.send(h, 2, 0, "all", 0, -1)
            self.hand_on(h, 2, 0)

    def turn(self, i):
        for s in (-1, 1):
            for h in (0, 1):
                self.arrive(h, i, s, "all")
                self.forward(h, i, s)
                self.hand_on(h, i, s)

    def last(self, i):
        for h in (0, 1):
            for part in ("first", "second"):
                self.arrive(h, i, 2, part)
            self.hand_on(h, i, 2)

    def all_here(self):
        for _, coming in self.near:
            coming.wait_recv()

    def drain(self):
        for copy in self.sends:
            copy.wait_send()
        for copy, _ in self.near:
            copy.wait_send()


class Reduce:
    def __init__(self, c, ptr, run, o_ref, sent, got, sent_scale, got_scale, sems):
        self.row, self.me, self.ring = lax.axis_index("row"), lax.axis_index("col"), lax.axis_size("col")
        self.c, self.ptr, self.run, self.o_ref = c, ptr, run, o_ref
        self.sent, self.got, self.sent_scale, self.got_scale, self.sems = sent, got, sent_scale, got_scale, sems
        self.side = run.shape[2]
        self.blocks = o_ref.shape[0] // self.side
        self.started = []

    def at(self, offset):
        return lax.rem(self.me + offset + self.ring, self.ring)

    def copies(self, w, k):
        send_sem, recv_sem, scale_send, scale_recv = self.sems
        c = self.c
        return [
            pltpu.make_async_remote_copy(
                src_ref=a.at[c, w, k],
                dst_ref=b.at[c, w, k],
                send_sem=s.at[c, w, k],
                recv_sem=r.at[c, w, k],
                device_id=(self.row, self.at(1 - 2 * w)),
                device_id_type=MESH,
            )
            for a, b, s, r in (
                (self.sent, self.got, send_sem, recv_sem),
                (self.sent_scale, self.got_scale, scale_send, scale_recv),
            )
        ]

    def partial(self, offset, h, j):
        i = self.at(offset) * self.blocks + h * (self.blocks // 2) + j
        end = self.ptr[i + 1]
        return self.run[self.c, jnp.where(end > self.ptr[i], end, 0)]

    def spread(self, w, k, j):
        span = pl.ds(pl.multiple_of(j * self.side, self.side), self.side)
        return self.got[self.c, w, k, span, :].astype(jnp.int32).astype(jnp.float32) * self.got_scale[self.c, w, k, pl.ds(j, 1), :]

    def step(self, k):
        for w in (0, 1):
            offset, h = (1 - 2 * w) * (self.ring // 2 - (k + 1) // 2), w if k % 2 == 0 else 1 - w
            if k >= 2:
                for copy in self.copies(w, k - 2):
                    copy.wait_recv()

            def code(j, carry, w=w, offset=offset, h=h):
                value = self.partial(offset, h, j)
                if k >= 2:
                    value = value + self.spread(w, k - 2, j)
                top = jnp.maximum(jnp.max(jnp.abs(value), axis=0, keepdims=True), 1e-30)
                self.sent_scale[self.c, w, k, pl.ds(j, 1), :] = top * (1.0 / LIMIT)
                span = pl.ds(pl.multiple_of(j * self.side, self.side), self.side)
                self.sent[self.c, w, k, span, :] = jnp.round(value * (LIMIT / top)).astype(jnp.int32).astype(jnp.int16)
                return carry

            lax.fori_loop(0, self.blocks // 2, code, 0)
            for copy in self.copies(w, k):
                copy.start()
                self.started.append(copy)

    def finish(self):
        last = self.ring - 2
        for k in (last - 1, last):
            for w in (0, 1):
                for copy in self.copies(w, k):
                    copy.wait_recv()
        lanes = self.run.shape[3]
        for h in (0, 1):

            def add(j, carry, h=h):
                value = self.partial(0, h, j) + (self.spread(h, last, j) + self.spread(1 - h, last - 1, j))
                start = (h * (self.blocks // 2) + j) * self.side
                span = pl.ds(pl.multiple_of(start, self.side), self.side)
                self.o_ref[span, pl.ds(self.c * lanes, lanes)] = value.astype(self.o_ref.dtype)
                return carry

            lax.fori_loop(0, self.blocks // 2, add, 0)

    def drain(self):
        for copy in self.started:
            copy.wait_send()


def kernel(
    ptr, cols, ptr_row, x_ref, a_ref, o_ref,
    panel_one, panel_two, values, run, same, sent, got, sent_scale, got_scale,
    load_sem, link_send, link_recv, near_send, near_recv, send_sem, recv_sem, scale_send, scale_recv,
):
    row, col = lax.axis_index("row"), lax.axis_index("col")
    panels = (panel_one, panel_two)
    blocks, side, lanes = panel_one.shape
    depth = blocks // lax.axis_size("row")

    loads = [
        pltpu.make_async_copy(
            x_ref.at[:, :, pl.ds(c * lanes, lanes)], panels[c].at[pl.ds(row * depth, depth)], load_sem.at[c]
        )
        for c in (0, 1)
    ] + [pltpu.make_async_copy(a_ref.at[pl.ds(0, ROOM)], values, load_sem.at[2])]
    for load in loads:
        load.start()

    gathers = [Gather(c, panels, link_send, link_recv, near_send, near_recv) for c in (0, 1)]
    sems = (send_sem, recv_sem, scale_send, scale_recv)
    sums = [Reduce(c, ptr, run, o_ref, sent, got, sent_scale, got_scale, sems) for c in (0, 1)]
    g, r = gathers[0], sums[0]
    barrier = pltpu.get_barrier_semaphore()
    neighbours = [(g.rank(0, i, j), col) for i, j in ((1, 0), (-1, 0), (0, 1), (0, -1))]
    neighbours += [(g.rank(0, 0, 0, True), col), (row, r.at(1)), (row, r.at(-1))]
    for device in neighbours:
        pl.semaphore_signal(barrier, inc=1, device_id=device, device_id_type=MESH)
    pl.semaphore_wait(barrier, len(neighbours))

    def multiply(c, first, last):
        def step(n, carry):
            total = run[c, n * GROUP]
            for u in range(GROUP):
                s = n * GROUP + u
                product = jnp.dot(values[s], panels[c][lax.rem(cols[s], blocks)], preferred_element_type=jnp.float32)
                total = total * same[pl.ds(s, 1), :] + product
                run[c, s + 1] = total
            return carry

        lax.fori_loop(first, last, step, 0)

    halfway, whole = ROOM // GROUP // 2, ROOM // GROUP
    one, two = gathers
    sum1, sum2 = sums

    loads[0].wait()
    one.own()
    loads[1].wait()
    starts = jnp.max(
        (lax.broadcasted_iota(jnp.int32, (ROOM, ptr_row.shape[1]), 0) == ptr_row[...]).astype(jnp.float32), axis=1, keepdims=True
    )
    same[...] = jnp.broadcast_to(1.0 - starts, same.shape)
    for c in (0, 1):
        run[c, 0] = jnp.zeros((side, lanes), jnp.float32)
    loads[2].wait()
    one.first_hop()
    one.turn(0)
    one.second_hop()
    one.turn(-1)
    one.turn(1)
    one.turn(2)
    two.own()
    for i in (0, -1, 1, 2):
        one.last(i)
    one.all_here()
    multiply(0, 0, halfway)
    two.first_hop()
    multiply(0, halfway, whole)
    sum1.step(0)
    sum1.step(1)
    two.turn(0)
    two.second_hop()
    two.turn(-1)
    sum1.step(2)
    two.turn(1)
    sum1.step(3)
    sum1.step(4)
    two.turn(2)
    for i in (0, -1, 1):
        two.last(i)
    sum1.step(5)
    two.last(2)
    two.all_here()
    multiply(1, 0, halfway)
    sum1.step(6)
    multiply(1, halfway, whole)
    sum2.step(0)
    sum2.step(1)
    sum1.finish()
    for k in range(2, 7):
        sum2.step(k)
    sum2.finish()
    for stream in (*gathers, *sums):
        stream.drain()


def local(features, block_values, row_ptr, block_cols):
    values, pointers, columns = block_values[0, 0], row_ptr[0, 0], block_cols[0, 0]
    side = values.shape[1]
    ranks, ring = lax.axis_size("row"), lax.axis_size("col")
    depth, width = features.shape
    lanes = width // 2
    blocks = ranks * depth // side
    owned = (pointers.shape[0] - 1) * side // ring
    steps = ring - 1
    return pl.pallas_call(
        kernel,
        out_shape=jax.ShapeDtypeStruct((owned, width), jnp.bfloat16),
        in_specs=[
            pl.BlockSpec(memory_space=pltpu.SMEM),
            pl.BlockSpec(memory_space=pltpu.SMEM),
            pl.BlockSpec(memory_space=pltpu.VMEM),
            pl.BlockSpec(memory_space=pl.ANY),
            pl.BlockSpec(memory_space=pl.ANY),
        ],
        out_specs=pl.BlockSpec(memory_space=pltpu.VMEM),
        scratch_shapes=[
            pltpu.VMEM((blocks, side, lanes), jnp.bfloat16),
            pltpu.VMEM((blocks, side, lanes), jnp.bfloat16),
            pltpu.VMEM((ROOM, side, side), jnp.bfloat16),
            pltpu.VMEM((2, ROOM + 1, side, lanes), jnp.float32),
            pltpu.VMEM((ROOM, lanes), jnp.float32),
            pltpu.VMEM((2, 2, steps, owned // 2, lanes), jnp.int16),
            pltpu.VMEM((2, 2, steps, owned // 2, lanes), jnp.int16),
            pltpu.VMEM((2, 2, steps, owned // side // 2, lanes), jnp.float32),
            pltpu.VMEM((2, 2, steps, owned // side // 2, lanes), jnp.float32),
            pltpu.SemaphoreType.DMA((3,)),
            pltpu.SemaphoreType.DMA((2, LINKS)),
            pltpu.SemaphoreType.DMA((2, LINKS)),
            pltpu.SemaphoreType.DMA((2, CROSSINGS)),
            pltpu.SemaphoreType.DMA((2, CROSSINGS)),
            pltpu.SemaphoreType.DMA((2, 2, steps)),
            pltpu.SemaphoreType.DMA((2, 2, steps)),
            pltpu.SemaphoreType.DMA((2, 2, steps)),
            pltpu.SemaphoreType.DMA((2, 2, steps)),
        ],
        compiler_params=pltpu.CompilerParams(
            collective_id=0, has_side_effects=True, vmem_limit_bytes=60 * 1024 * 1024
        ),
        name="block_sparse",
    )(pointers, columns, pointers[None, :], features.reshape(depth // side, side, width), values)


def solution(mesh):
    return jax.shard_map(
        local,
        mesh=mesh,
        in_specs=(
            P(("col", "row"), None),
            P("row", "col", None, None, None),
            P("row", "col", None),
            P("row", "col", None),
        ),
        out_specs=P(("row", "col"), None),
        check_vma=False,
    )
```

time: 272 us -> 93 us (0.34)
  waiting for transfers between devices: 178 us -> 0 us
  Pallas kernels: 0 us -> 90.9 us
  local copies, waits for them, and re-layouts: 47.8 us -> 1.87 us
  matrix products: 29.5 us -> 0 us
  between operations: 13.4 us -> 0.01 us
  other arithmetic: 2.76 us -> 0 us
    reduce_scatter x1 -> x0, waiting for transfers between devices: 94.2 us -> none  [local(): lax.psum_scatter(partial_value, 'col', scatter_dimension=0, tiled=True)]
    pallas_call x0 -> x1, Pallas kernels: none -> 90.9 us  [local(): pl.pallas_call(kernel, out_shape=jax.ShapeDtypeStruct((owned, width), jnp...]
    all_gather x1 -> x0, waiting for transfers between devices: 82.9 us -> none  [local(): panel = lax.all_gather(features, 'row', axis=0, tiled=True)]
    dot_general x2 -> x0, local copies, waits for them, and re-layouts: 33 us -> none  [the longest x1 24.9 us: local(): jnp.einsum('sij,sjk->sik', values, blocks, preferred_element_type=jnp.flo...]
    dot_general x2 -> x0, matrix products: 29.5 us -> none  [the longest x1 15.7 us: local(): jnp.einsum('rs,sik->rik', weights, products, precision=lax.Precision.HIGH...]
    gather x1 -> x0, local copies, waits for them, and re-layouts: 14.1 us -> none  [local(): blocks = panel_blocks[columns]]
  transfers between devices with their start and end apart: 2 -> 0, of which waited for: 2 -> 0; matrix products, arithmetic and copies ran while one was open for 1% -> 0% of each run, Pallas kernels for 0% -> 0%
where the time goes in v2:
time: 93 us; the launch traced here: 92.8 us
  Pallas kernels  90.9 us (98%)
  local copies, waits for them, and re-layouts  1.87 us (2%)
    pallas_call x1, Pallas kernels, local(): pl.pallas_call(kernel, out_shape=jax.ShapeDtypeStruct((owned, width), jnp...  90.9 us
    unnamed x1, local copies, waits for them, and re-layouts  1.87 us

profile of v2, /device:TPU:1, one launch (start us, length us, event | category | flops | bytes accessed | tf_op | source)
XLA Modules:
  0.0 92.8 jit_solution(2376888814568130726)
XLA Ops:
  0.0 90.9 %block_sparse.1 = bf16[1024,256]{1,0:T(8,128)(2,1)} custom-call(s32[65]{0:T(128)} %bitcast.7, s32[192]{0:T(256)} %bitcast.9, s32[1,65]{1,0:T(1,128)} %bitcast.8, bf16[8,128,256]{2,1,0:T(8,128)(2,1)} %bitcast.6, bf16[192,128,128]{2,1,0:T(8,128)(2,1)} %bitcast.5), custom_call_target="tpu_custom_call" | custom-call | tf_op jit(solution)/shard_map/block_sparse/pallas_call | solution.py:318
  91.0 1.9 %copy.6 = bf16[1024,256]{1,0:T(8,128)(2,1)} copy(bf16[1024,256]{1,0:T(8,128)(2,1)} %block_sparse.1) | data formatting | bytes 1048576

commit v3 on v0

v3 whole, which is shorter than its diff:
```python
import jax
import jax.numpy as jnp
from jax import lax
from jax.experimental import pallas as pl
from jax.experimental.pallas import tpu as pltpu
from jax.sharding import PartitionSpec as P

MESH = pl.DeviceIdType.MESH
SIDE = 4
GROUP = 8
ROOM = 144
LIMIT = 32767.0
CHUNKS = 4
EVENTS = 10
PARTS = 6
SUMS = 3


class Gather:
    def __init__(self, c, panels, send_sem, recv_sem, near_recv):
        me, self.col = lax.axis_index("row"), lax.axis_index("col")
        self.c, self.panel = c, panels[c]
        self.core, self.x, self.y = lax.rem(me, 2), lax.rem(me // 2, SIDE), me // (2 * SIDE)
        self.depth = self.panel.shape[0] // lax.axis_size("row")
        self.send_sem, self.recv_sem, self.near_recv = send_sem.at[c], recv_sem, near_recv.at[c]
        self.sent, self.due, self.near = 0, [0] * EVENTS, 0

    def rank(self, h, i, j, other=False):
        dx, dy = (i, j) if h == 0 else (j, i)
        core = 1 - self.core if other else self.core
        return (lax.rem(self.y + dy + SIDE, SIDE) * SIDE + lax.rem(self.x + dx + SIDE, SIDE)) * 2 + core

    def piece(self, h, i, j, part, other=False):
        half, quarter = self.depth // 2, self.depth // 4
        first, size = {"all": (0, half), "first": (0, quarter), "second": (quarter, quarter)}[part]
        return self.panel.at[pl.ds(self.rank(h, i, j, other) * self.depth + h * half + first, size)]

    def event(self, i, j):
        i, j = (i + 1) % SIDE - 1, (j + 1) % SIDE - 1
        return {0: 0 if i != 2 else 1, 2: 6 + i + 1}.get(j, 2 + i + 1)

    def start(self, ref, recv_sem, device):
        pltpu.make_async_remote_copy(
            src_ref=ref,
            dst_ref=ref,
            send_sem=self.send_sem,
            recv_sem=recv_sem,
            device_id=(device, self.col),
            device_id_type=MESH,
        ).start()
        self.sent += ref.shape[0]
        return ref.shape[0]

    def blocks(self, count, recv_sem):
        ref = self.panel.at[pl.ds(0, count)]
        return pltpu.make_async_remote_copy(
            src_ref=ref,
            dst_ref=ref,
            send_sem=self.send_sem,
            recv_sem=recv_sem,
            device_id=(self.rank(0, 0, 0, True), self.col),
            device_id_type=MESH,
        )

    def send(self, h, i, j, part, di, dj):
        event = self.event(i - di, j - dj)
        self.due[event] += self.start(self.piece(h, i, j, part), self.recv_sem.at[self.c, event], self.rank(h, di, dj))

    def arrive(self, i, j):
        event = self.event(i, j)
        self.blocks(self.due[event], self.recv_sem.at[self.c, event]).wait_recv()

    def hand_on(self, h, i, j):
        self.near += self.start(self.piece(h, i, j, "all"), self.near_recv, self.rank(0, 0, 0, True))

    def own(self):
        for di, dj in ((1, 0), (-1, 0), (0, 1), (0, -1)):
            for h in (0, 1):
                self.send(h, 0, 0, "all", di, dj)
        mine = self.panel.at[pl.ds(self.rank(0, 0, 0) * self.depth, self.depth)]
        self.near += self.start(mine, self.near_recv, self.rank(0, 0, 0, True))

    def forward(self, h, i, j):
        self.send(h, i, j, "first" if j == -1 else "second", 0, -j)

    def first_hop(self):
        pieces = [(h, s) for s in (-1, 1) for h in (0, 1)]
        self.arrive(1, 0)
        for h, s in pieces:
            self.send(h, s, 0, "first" if s == -1 else "second", -s, 0)
        for h, s in pieces:
            self.send(h, s, 0, "all", 0, 1)
            self.send(h, s, 0, "all", 0, -1)
        for h, s in pieces:
            self.hand_on(h, s, 0)

    def second_hop(self):
        self.arrive(2, 0)
        for h in (0, 1):
            self.send(h, 2, 0, "all", 0, 1)
            self.send(h, 2, 0, "all", 0, -1)
            self.hand_on(h, 2, 0)

    def turn(self, i):
        self.arrive(i, 1)
        for s in (-1, 1):
            for h in (0, 1):
                self.forward(h, i, s)
        for s in (-1, 1):
            for h in (0, 1):
                self.hand_on(h, i, s)

    def last(self, i):
        self.arrive(i, 2)
        for h in (0, 1):
            self.hand_on(h, i, 2)

    def tail(self):
        for i in (0, -1, 1, 2):
            self.last(i)

    def all_here(self):
        self.blocks(self.near, self.near_recv).wait_recv()

    def drain(self):
        self.blocks(self.sent, self.near_recv).wait_send()


class Reduce:
    def __init__(self, c, ptr, run, o_ref, held, sent, got, sent_scale, got_scale, sems):
        self.row, self.me, self.ring = lax.axis_index("row"), lax.axis_index("col"), lax.axis_size("col")
        self.c, self.ptr, self.run, self.o_ref, self.held = c, ptr, run, o_ref, held
        self.sent, self.got, self.sent_scale, self.got_scale, self.sems = sent, got, sent_scale, got_scale, sems
        self.side, self.lanes = run.shape[2:]
        self.pairs = o_ref.shape[0] // self.side // 2
        self.low = lax.broadcasted_iota(jnp.int32, (self.side, self.lanes), 1) < self.lanes // 2

    def at(self, offset):
        return lax.rem(self.me + offset + self.ring, self.ring)

    def copies(self, w, *refs_and_sems):
        for a, b, s, r in refs_and_sems:
            yield pltpu.make_async_remote_copy(
                src_ref=a,
                dst_ref=b,
                send_sem=s,
                recv_sem=r,
                device_id=(self.row, self.at(1 - 2 * w)),
                device_id_type=MESH,
            )

    def both(self, at, k, j=0):
        send_sem, recv_sem, scale_send, scale_recv = self.sems
        at = (self.c, *at)
        r = self.c + j
        return (
            (self.sent.at[at], self.got.at[at], send_sem.at[self.c], recv_sem.at[r, k]),
            (self.sent_scale.at[at], self.got_scale.at[at], scale_send.at[self.c], scale_recv.at[r, k]),
        )

    def arrive(self, k, j=None):
        at = (0, pl.ds(0, 2)) if j is None else (0, 0)
        for copy in self.copies(0, *self.both(at, k, j or 0)):
            copy.wait_recv()

    def total(self, i):
        end = self.ptr[i + 1]
        return self.run[self.c % SUMS, jnp.where(end > self.ptr[i], end, 0)]

    def partial(self, offset, h, j):
        i = (self.at(offset) * self.pairs + h * (self.pairs // 2) + j) * 2
        one, two = self.total(i), self.total(i + 1)
        return jnp.where(self.low, one, two) + self.swap(jnp.where(self.low, two, one))

    def swap(self, value):
        return pltpu.roll(value, self.lanes // 2, 1)

    def spread(self, w, k, j):
        return self.got[self.c, w, k, j].astype(jnp.int32).astype(jnp.float32) * self.got_scale[self.c, w, k, j]

    def encode(self, k, j):
        for w in (0, 1):
            offset, h = (1 - 2 * w) * (self.ring // 2 - (k + 1) // 2), w if k % 2 == 0 else 1 - w
            value = self.partial(offset, h, j)
            if k >= 2:
                value = value + self.spread(w, k - 2, j)
            top = jnp.maximum(jnp.max(jnp.abs(value), axis=0, keepdims=True), 1e-30)
            self.sent_scale[self.c, w, k, j] = top * (1.0 / LIMIT)
            self.sent[self.c, w, k, j] = jnp.round(value * (LIMIT / top)).astype(jnp.int32).astype(jnp.int16)

    def start(self, k, j=None):
        for w in (0, 1):
            for copy in self.copies(w, *self.both((w, k) if j is None else (w, k, j), k, j or 0)):
                copy.start()

    def step(self, k):
        if k >= 2:
            self.arrive(k - 2)
        for j in range(self.pairs // 2):
            self.encode(k, j)
        self.start(k)

    def half_step(self, k):
        for j in range(self.pairs // 2):
            if k >= 2:
                self.arrive(k - 2, j)
            self.encode(k, j)
            self.start(k, j)

    def finish(self, halves=False):
        last = self.ring - 2
        if not halves:
            self.arrive(last - 1)
            self.arrive(last)
        for j in range(self.pairs // 2):
            if halves:
                self.arrive(last - 1, j)
                self.arrive(last, j)
            for h in (0, 1):
                value = self.partial(0, h, j) + (self.spread(h, last, j) + self.spread(1 - h, last - 1, j))
                n = h * (self.pairs // 2) + j
                if self.c % 2 == 0:
                    self.held[n] = value
                else:
                    before = self.held[n]
                    both = jnp.where(self.low, before, self.swap(value)), jnp.where(self.low, self.swap(before), value)
                    for u in (0, 1):
                        span = pl.ds((2 * n + u) * self.side, self.side)
                        self.o_ref[span, pl.ds(self.c // 2 * self.lanes, self.lanes)] = both[u].astype(self.o_ref.dtype)

    def drain(self):
        for copy in self.copies(0, *self.both((), 0)):
            copy.wait_send()


def kernel(
    ptr_ref, cols_ref, ptr_row_ref, cols_row_ref, x_ref, a_ref, o_ref,
    ptr, cols, ptr_row, cols_row, panel_0, panel_1, panel_2, panel_3, own, values, run, same, mine, held, sent, got, sent_scale, got_scale,
    load_sem, link_send, link_recv, near_recv, send_sem, recv_sem, scale_send, scale_recv,
):
    row, col = lax.axis_index("row"), lax.axis_index("col")
    panels = (panel_0, panel_1, panel_2, panel_3)
    pairs, side, lanes = panel_0.shape
    depth = pairs // lax.axis_size("row")

    load = pltpu.make_async_copy(x_ref, own, load_sem.at[0])
    load_values = pltpu.make_async_copy(a_ref.at[pl.ds(0, ROOM)], values, load_sem.at[1])
    small = [
        pltpu.make_async_copy(a, b, load_sem.at[2 + n])
        for n, (a, b) in enumerate(((ptr_ref, ptr), (cols_ref, cols), (ptr_row_ref, ptr_row), (cols_row_ref, cols_row)))
    ]
    for copy in (load, *small, load_values):
        copy.start()

    gathers = [Gather(c, panels, link_send, link_recv, near_recv) for c in range(CHUNKS)]
    sems = (send_sem, recv_sem, scale_send, scale_recv)
    sums = [Reduce(c, ptr, run, o_ref, held, sent, got, sent_scale, got_scale, sems) for c in range(CHUNKS)]
    g, r = gathers[0], sums[0]
    barrier = pltpu.get_barrier_semaphore()
    neighbours = [(g.rank(0, i, j), col) for i, j in ((1, 0), (-1, 0), (0, 1), (0, -1))]
    neighbours += [(g.rank(0, 0, 0, True), col), (row, r.at(1)), (row, r.at(-1))]
    for device in neighbours:
        pl.semaphore_signal(barrier, inc=1, device_id=device, device_id_type=MESH)

    def pack(c):
        for n in range(depth):
            cut = pl.ds(c // 2 * lanes, lanes)
            one, two = (own[2 * n + u, :, cut].astype(jnp.float32) for u in (0, 1))
            if c % 2 == 0:
                two = r.swap(two)
            else:
                one = r.swap(one)
            panels[c][row * depth + n] = jnp.where(r.low, one, two).astype(jnp.bfloat16)

    load.wait()
    pack(0)
    pl.semaphore_wait(barrier, len(neighbours))
    gathers[0].own()
    for c in range(1, CHUNKS):
        pack(c)
    for copy in small:
        copy.wait()
    shape = (ROOM, ptr_row.shape[1])
    starts = jnp.max((lax.broadcasted_iota(jnp.int32, shape, 0) == ptr_row[...]).astype(jnp.float32), axis=1, keepdims=True)
    same[...] = jnp.broadcast_to(1.0 - starts, same.shape)
    shape = (ROOM, cols_row.shape[1])
    slot = lax.broadcasted_iota(jnp.int32, shape, 0) == lax.broadcasted_iota(jnp.int32, shape, 1)
    odd = jnp.max(jnp.where(slot, lax.rem(cols_row[...], 2), 0).astype(jnp.float32), axis=1, keepdims=True)
    high = (lax.broadcasted_iota(jnp.int32, mine.shape, 1) >= lanes // 2).astype(jnp.float32)
    mine[...] = high * odd + (1.0 - high) * (1.0 - odd)
    for n in range(SUMS):
        run[n, 0] = jnp.zeros((side, lanes), jnp.float32)

    def multiply(c, first, last):
        def step(n, carry):
            total = run[c % SUMS, n * GROUP]
            for u in range(GROUP):
                s = n * GROUP + u
                pair = lax.div(lax.rem(cols[s], 2 * pairs), 2)
                product = jnp.dot(values[s], panels[c][pair], preferred_element_type=jnp.float32)
                total = total * same[pl.ds(s, 1), :] + product * mine[pl.ds(s, 1), :]
                run[c % SUMS, s + 1] = total
            return carry

        lax.fori_loop(first, last, step, 0)

    share = ROOM // GROUP // PARTS

    def work(c, *parts):
        for part in parts:
            multiply(c, part * share, (part + 1) * share)

    def take(n, *names):
        for name in names:
            if isinstance(name, int):
                gathers[n].turn(name)
            else:
                getattr(gathers[n], name)()

    def add(n, *steps):
        for k in steps:
            sums[n].step(k)

    load_values.wait()
    take(0, "first_hop", 0, "second_hop")
    take(1, "own")
    take(0, -1, 1, 2)
    take(1, "first_hop", 0)
    take(0, "tail")
    take(1, "second_hop")
    take(2, "own")
    take(0, "all_here")
    work(0, 0)
    take(1, -1)
    work(0, 1)
    take(1, 1)
    work(0, 2, 3)
    take(1, 2)
    work(0, 4)
    take(2, "first_hop")
    work(0, 5)
    add(0, 0, 1)
    take(2, 0)
    take(1, "tail")
    take(2, "second_hop")
    take(3, "own")
    add(0, 2)
    take(1, "all_here")
    work(1, 0)
    take(2, -1)
    add(0, 3)
    work(1, 1)
    take(2, 1)
    work(1, 2, 3)
    take(2, 2)
    work(1, 4)
    add(0, 4)
    work(1, 5)
    take(3, "first_hop")
    add(0, 5)
    add(1, 0, 1)
    take(3, 0)
    take(2, "tail")
    take(3, "second_hop")
    add(0, 6)
    take(2, "all_here")
    take(3, -1)
    work(2, 0)
    take(3, 1)
    add(1, 2)
    work(2, 1)
    add(1, 3)
    work(2, 2)
    take(3, 2)
    work(2, 3)
    sums[0].finish()
    work(2, 4)
    add(1, 4)
    work(2, 5)
    add(2, 0, 1)
    add(1, 5)
    take(3, "tail", "all_here")
    work(3, 0)
    add(1, 6)
    work(3, 1)
    add(2, 2)
    work(3, 2)
    add(2, 3)
    work(3, 3, 4)
    sums[1].finish()
    work(3, 5)
    last = sums[3]
    last.half_step(0)
    last.half_step(1)
    add(2, 4, 5)
    for stream in (*gathers, *sums[:2]):
        stream.drain()
    last.half_step(2)
    last.half_step(3)
    add(2, 6)
    last.half_step(4)
    last.half_step(5)
    sums[2].finish()
    sums[2].drain()
    last.half_step(6)
    last.finish(True)
    last.drain()


def local(features, block_values, row_ptr, block_cols):
    values, pointers, columns = block_values[0, 0], row_ptr[0, 0], block_cols[0, 0]
    side = values.shape[1]
    ranks, ring = lax.axis_size("row"), lax.axis_size("col")
    depth, width = features.shape
    lanes = 2 * width // CHUNKS
    pairs = ranks * depth // side // 2
    owned = (pointers.shape[0] - 1) * side // ring
    steps = ring - 1
    half = owned // 4
    return pl.pallas_call(
        kernel,
        out_shape=jax.ShapeDtypeStruct((owned, width), jnp.bfloat16),
        in_specs=[
            pl.BlockSpec(memory_space=pltpu.HBM),
            pl.BlockSpec(memory_space=pltpu.HBM),
            pl.BlockSpec(memory_space=pltpu.HBM),
            pl.BlockSpec(memory_space=pltpu.HBM),
            pl.BlockSpec(memory_space=pltpu.HBM),
            pl.BlockSpec(memory_space=pltpu.HBM),
        ],
        out_specs=pl.BlockSpec(memory_space=pltpu.VMEM),
        scratch_shapes=[
            pltpu.SMEM(pointers.shape, jnp.int32),
            pltpu.SMEM(columns.shape, jnp.int32),
            pltpu.VMEM((1, *pointers.shape), jnp.int32),
            pltpu.VMEM((1, *columns.shape), jnp.int32),
        ]
        + [pltpu.VMEM((pairs, side, lanes), jnp.bfloat16)] * CHUNKS
        + [
            pltpu.VMEM((depth // side, side, width), jnp.bfloat16),
            pltpu.VMEM((ROOM, side, side), jnp.bfloat16),
            pltpu.VMEM((SUMS, ROOM + 1, side, lanes), jnp.float32),
            pltpu.VMEM((ROOM, lanes), jnp.float32),
            pltpu.VMEM((ROOM, lanes), jnp.float32),
            pltpu.VMEM((owned // side // 2, side, lanes), jnp.float32),
            pltpu.VMEM((CHUNKS, 2, steps, half // side, side, lanes), jnp.int16),
            pltpu.VMEM((CHUNKS, 2, steps, half // side, side, lanes), jnp.int16),
            pltpu.VMEM((CHUNKS, 2, steps, half // side, 1, lanes), jnp.float32),
            pltpu.VMEM((CHUNKS, 2, steps, half // side, 1, lanes), jnp.float32),
            pltpu.SemaphoreType.DMA((6,)),
            pltpu.SemaphoreType.DMA((CHUNKS,)),
            pltpu.SemaphoreType.DMA((CHUNKS, EVENTS)),
            pltpu.SemaphoreType.DMA((CHUNKS,)),
            pltpu.SemaphoreType.DMA((CHUNKS,)),
            pltpu.SemaphoreType.DMA((CHUNKS + 1, steps)),
            pltpu.SemaphoreType.DMA((CHUNKS,)),
            pltpu.SemaphoreType.DMA((CHUNKS + 1, steps)),
        ],
        compiler_params=pltpu.CompilerParams(
            collective_id=0, has_side_effects=True, vmem_limit_bytes=58 * 1024 * 1024
        ),
        name="block_sparse",
    )(pointers, columns, pointers[None, :], columns[None, :], features.reshape(depth // side, side, width), values)


def solution(mesh):
    return jax.shard_map(
        local,
        mesh=mesh,
        in_specs=(
            P(("col", "row"), None),
            P("row", "col", None, None, None),
            P("row", "col", None),
            P("row", "col", None),
        ),
        out_specs=P(("row", "col"), None),
        check_vma=False,
    )
```

time: 272 us -> 85.8 us (0.32)
  waiting for transfers between devices: 178 us -> 0 us
  Pallas kernels: 0 us -> 82.3 us
  local copies, waits for them, and re-layouts: 47.8 us -> 1.87 us
  matrix products: 29.5 us -> 0 us
  between operations: 13.4 us -> 0.01 us
  other arithmetic: 2.76 us -> 0 us
    reduce_scatter x1 -> x0, waiting for transfers between devices: 94.2 us -> none  [local(): lax.psum_scatter(partial_value, 'col', scatter_dimension=0, tiled=True)]
    all_gather x1 -> x0, waiting for transfers between devices: 82.9 us -> none  [local(): panel = lax.all_gather(features, 'row', axis=0, tiled=True)]
    pallas_call x0 -> x1, Pallas kernels: none -> 82.3 us  [local(): pl.pallas_call(kernel, out_shape=jax.ShapeDtypeStruct((owned, width), jnp...]
    dot_general x2 -> x0, local copies, waits for them, and re-layouts: 33 us -> none  [the longest x1 24.9 us: local(): jnp.einsum('sij,sjk->sik', values, blocks, preferred_element_type=jnp.flo...]
    dot_general x2 -> x0, matrix products: 29.5 us -> none  [the longest x1 15.7 us: local(): jnp.einsum('rs,sik->rik', weights, products, precision=lax.Precision.HIGH...]
    gather x1 -> x0, local copies, waits for them, and re-layouts: 14.1 us -> none  [local(): blocks = panel_blocks[columns]]
  transfers between devices with their start and end apart: 2 -> 0, of which waited for: 2 -> 0; matrix products, arithmetic and copies ran while one was open for 1% -> 0% of each run, Pallas kernels for 0% -> 0%
where the time goes in v3:
time: 85.8 us; the launch traced here: 84.2 us
  Pallas kernels  82.3 us (96%)
  local copies, waits for them, and re-layouts  1.87 us (2%)
    pallas_call x1, Pallas kernels, local(): pl.pallas_call(kernel, out_shape=jax.ShapeDtypeStruct((owned, width), jnp...  82.3 us
    unnamed x1, local copies, waits for them, and re-layouts  1.87 us

profile of v3, /device:TPU:1, one launch (start us, length us, event | category | flops | bytes accessed | tf_op | source)
XLA Modules:
  0.0 84.2 jit_solution(15300364509162101585)
XLA Ops:
  0.0 82.3 %block_sparse.1 = bf16[1024,256]{1,0:T(8,128)(2,1)} custom-call(s32[65]{0:T(128)} %bitcast.10, s32[192]{0:T(256)} %bitcast.8, s32[1,65]{1,0:T(1,128)} %bitcast.11, s32[1,192]{1,0:T(1,128)} %bitcast.9, bf16[8,128,256]{2,1,0:T(8,128)(2,1)} %bitcast.7, bf16[192,128,128]{2,1,0:T(8,128)(2,1)} %bitcast.6), custom_call_target="tpu_custom_call" | custom-call | tf_op jit(solution)/shard_map/block_sparse/pallas_call | solution.py:420
  82.3 1.9 %copy.6 = bf16[1024,256]{1,0:T(8,128)(2,1)} copy(bf16[1024,256]{1,0:T(8,128)(2,1)} %block_sparse.1) | data formatting | bytes 1048576

commit v4 on v3

--- a/solution.py
+++ b/solution.py
@@ -13,7 +13,7 @@
 CHUNKS = 4
 EVENTS = 10
 PARTS = 6
-SUMS = 3
+SUMS = 2
 
 
 class Gather:
@@ -101,23 +101,27 @@
             self.send(h, 2, 0, "all", 0, -1)
             self.hand_on(h, 2, 0)
 
-    def turn(self, i):
+    def turn(self, i, direct=False):
         self.arrive(i, 1)
         for s in (-1, 1):
             for h in (0, 1):
                 self.forward(h, i, s)
+                if direct:
+                    part = self.piece(h, i, s, "first" if s == -1 else "second")
+                    self.near += self.start(part, self.near_recv, self.rank(h, 0, -s, True))
         for s in (-1, 1):
             for h in (0, 1):
                 self.hand_on(h, i, s)
 
-    def last(self, i):
+    def last(self, i, direct=False):
         self.arrive(i, 2)
-        for h in (0, 1):
-            self.hand_on(h, i, 2)
-
-    def tail(self):
+        if not direct:
+            for h in (0, 1):
+                self.hand_on(h, i, 2)
+
+    def tail(self, direct=False):
         for i in (0, -1, 1, 2):
-            self.last(i)
+            self.last(i, direct and i == 2)
 
     def all_here(self):
         self.blocks(self.near, self.near_recv).wait_recv()
@@ -133,6 +137,7 @@
         self.sent, self.got, self.sent_scale, self.got_scale, self.sems = sent, got, sent_scale, got_scale, sems
         self.side, self.lanes = run.shape[2:]
         self.pairs = o_ref.shape[0] // self.side // 2
+        self.kept = {}
         self.low = lax.broadcasted_iota(jnp.int32, (self.side, self.lanes), 1) < self.lanes // 2
 
     def at(self, offset):
@@ -167,7 +172,16 @@
         end = self.ptr[i + 1]
         return self.run[self.c % SUMS, jnp.where(end > self.ptr[i], end, 0)]
 
+    def keep(self, stash, *places):
+        for offset, h in ((0, 0), (0, 1), *places):
+            for j in range(self.pairs // 2):
+                n = len(self.kept)
+                stash[n] = self.partial(offset, h, j)
+                self.kept[(offset, h, j)] = stash.at[n]
+
     def partial(self, offset, h, j):
+        if (offset, h, j) in self.kept:
+            return self.kept[(offset, h, j)][...]
         i = (self.at(offset) * self.pairs + h * (self.pairs // 2) + j) * 2
         one, two = self.total(i), self.total(i + 1)
         return jnp.where(self.low, one, two) + self.swap(jnp.where(self.low, two, one))
@@ -235,7 +249,7 @@
 
 def kernel(
     ptr_ref, cols_ref, ptr_row_ref, cols_row_ref, x_ref, a_ref, o_ref,
-    ptr, cols, ptr_row, cols_row, panel_0, panel_1, panel_2, panel_3, own, values, run, same, mine, held, sent, got, sent_scale, got_scale,
+    ptr, cols, ptr_row, cols_row, panel_0, panel_1, panel_2, panel_3, own, values, run, same, mine, held, early, late, sent, got, sent_scale, got_scale,
     load_sem, link_send, link_recv, near_recv, send_sem, recv_sem, scale_send, scale_recv,
 ):
     row, col = lax.axis_index("row"), lax.axis_index("col")
@@ -258,7 +272,8 @@
     g, r = gathers[0], sums[0]
     barrier = pltpu.get_barrier_semaphore()
     neighbours = [(g.rank(0, i, j), col) for i, j in ((1, 0), (-1, 0), (0, 1), (0, -1))]
-    neighbours += [(g.rank(0, 0, 0, True), col), (row, r.at(1)), (row, r.at(-1))]
+    neighbours += [(g.rank(0, i, j, True), col) for i, j in ((0, 0), (1, 0), (-1, 0), (0, 1), (0, -1))]
+    neighbours += [(row, r.at(1)), (row, r.at(-1))]
     for device in neighbours:
         pl.semaphore_signal(barrier, inc=1, device_id=device, device_id_type=MESH)
 
@@ -330,17 +345,15 @@
     take(1, "second_hop")
     take(2, "own")
     take(0, "all_here")
-    work(0, 0)
+    work(0, 0, 1)
     take(1, -1)
-    work(0, 1)
+    work(0, 2)
     take(1, 1)
-    work(0, 2, 3)
+    work(0, 3, 4)
     take(1, 2)
-    work(0, 4)
-    take(2, "first_hop")
     work(0, 5)
     add(0, 0, 1)
-    take(2, 0)
+    take(2, "first_hop", 0)
     take(1, "tail")
     take(2, "second_hop")
     take(3, "own")
@@ -357,52 +370,51 @@
     add(0, 4)
     work(1, 5)
     take(3, "first_hop")
+    add(1, 0, 1)
     add(0, 5)
-    add(1, 0, 1)
     take(3, 0)
     take(2, "tail")
     take(3, "second_hop")
     add(0, 6)
+    sums[0].keep(early)
     take(2, "all_here")
     take(3, -1)
     work(2, 0)
-    take(3, 1)
     add(1, 2)
     work(2, 1)
+    take(3, 1)
     add(1, 3)
-    work(2, 2)
-    take(3, 2)
-    work(2, 3)
+    work(2, 2, 3)
+    gathers[3].turn(2, True)
+    work(2, 4, 5)
+    add(2, 0, 1)
     sums[0].finish()
-    work(2, 4)
-    add(1, 4)
-    work(2, 5)
-    add(2, 0, 1)
-    add(1, 5)
-    take(3, "tail", "all_here")
-    work(3, 0)
-    add(1, 6)
-    work(3, 1)
+    add(1, 4, 5)
+    sums[1].keep(late, (1, 0), (-1, 1))
+    gathers[3].tail(True)
+    take(3, "all_here")
+    work(3, 0, 1)
     add(2, 2)
     work(3, 2)
+    add(1, 6)
     add(2, 3)
-    work(3, 3, 4)
-    sums[1].finish()
-    work(3, 5)
+    work(3, 3, 4, 5)
     last = sums[3]
     last.half_step(0)
     last.half_step(1)
-    add(2, 4, 5)
+    add(2, 4)
+    sums[1].finish()
     for stream in (*gathers, *sums[:2]):
         stream.drain()
     last.half_step(2)
     last.half_step(3)
+    add(2, 5)
+    last.half_step(4)
     add(2, 6)
-    last.half_step(4)
     last.half_step(5)
+    last.half_step(6)
     sums[2].finish()
     sums[2].drain()
-    last.half_step(6)
     last.finish(True)
     last.drain()
 
@@ -443,6 +455,8 @@
             pltpu.VMEM((ROOM, lanes), jnp.float32),
             pltpu.VMEM((ROOM, lanes), jnp.float32),
             pltpu.VMEM((owned // side // 2, side, lanes), jnp.float32),
+            pltpu.VMEM((owned // side // 2, side, lanes), jnp.float32),
+            pltpu.VMEM((owned // side, side, lanes), jnp.float32),
             pltpu.VMEM((CHUNKS, 2, steps, half // side, side, lanes), jnp.int16),
             pltpu.VMEM((CHUNKS, 2, steps, half // side, side, lanes), jnp.int16),
             pltpu.VMEM((CHUNKS, 2, steps, half // side, 1, lanes), jnp.float32),
@@ -457,10 +471,22 @@
             pltpu.SemaphoreType.DMA((CHUNKS + 1, steps)),
         ],
         compiler_params=pltpu.CompilerParams(
-            collective_id=0, has_side_effects=True, vmem_limit_bytes=58 * 1024 * 1024
+            collective_id=0, has_side_effects=True, vmem_limit_bytes=50 * 1024 * 1024
         ),
         name="block_sparse",
-    )(pointers, columns, pointers[None, :], columns[None, :], features.reshape(depth // side, side, width), values)
+    )(
+        *(
+            pltpu.with_memory_space_constraint(operand, pltpu.HBM)
+            for operand in (
+                pointers,
+                columns,
+                pointers[None, :],
+                columns[None, :],
+                features.reshape(depth // side, side, width),
+                values,
+            )
+        )
+    )
 
 
 def solution(mesh):

time: 85.8 us -> 82.7 us (0.964); the launches traced: 84.2 us -> 82.7 us
  local copies, waits for them, and re-layouts: 1.87 us -> 0.8 us
    unnamed x1, local copies, waits for them, and re-layouts: 1.87 us -> 0.8 us
where the time goes in v4:
time: 82.7 us
  Pallas kernels  81.9 us (99%)
    pallas_call x1, Pallas kernels, local(): pl.pallas_call(kernel, out_shape=jax.ShapeDtypeStruct((owned, width), jnp...  81.9 us

profile of v4, /device:TPU:1, one launch (start us, length us, event | category | flops | bytes accessed | tf_op | source)
XLA Modules:
  0.0 82.7 jit_solution(12558198463172506699)
XLA Ops:
  0.0 81.9 %block_sparse.1 = bf16[1024,256]{1,0:T(8,128)(2,1)S(1)} custom-call(s32[65]{0:T(128)} %bitcast.10, s32[192]{0:T(256)} %bitcast.8, s32[1,65]{1,0:T(1,128)} %bitcast.11, s32[1,192]{1,0:T(1,128)} %bitcast.9, bf16[8,128,256]{2,1,0:T(8,128)(2,1)} %bitcast.7, bf16[192,128,128]{2,1,0:T(8,128)(2,1)} %bitcast.6), custom_call_target="tpu_custom_call" | custom-call | tf_op jit(solution)/shard_map/block_sparse/pallas_call | solution.py:432
  81.9 0.8 copy.6

commit v5 on v4

--- a/solution.py
+++ b/solution.py
@@ -393,20 +393,21 @@
     sums[1].keep(late, (1, 0), (-1, 1))
     gathers[3].tail(True)
     take(3, "all_here")
-    work(3, 0, 1)
+    work(3, 0, 1, 2)
     add(2, 2)
-    work(3, 2)
+    work(3, 3)
     add(1, 6)
     add(2, 3)
-    work(3, 3, 4, 5)
+    work(3, 4, 5)
     last = sums[3]
     last.half_step(0)
     last.half_step(1)
     add(2, 4)
-    sums[1].finish()
-    for stream in (*gathers, *sums[:2]):
+    for stream in (*gathers, sums[0]):
         stream.drain()
     last.half_step(2)
+    sums[1].finish()
+    sums[1].drain()
     last.half_step(3)
     add(2, 5)
     last.half_step(4)

time: 82.7 us -> 82.5 us (level)
  no operation moved by 1% of the time
where the time goes in v5:
time: 82.5 us; the launch traced here: 82.4 us
  Pallas kernels  81.6 us (99%)
    pallas_call x1, Pallas kernels, local(): pl.pallas_call(kernel, out_shape=jax.ShapeDtypeStruct((owned, width), jnp...  81.6 us

profile of v5, /device:TPU:1, one launch (start us, length us, event | category | flops | bytes accessed | tf_op | source)
XLA Modules:
  0.0 82.4 jit_solution(17387117912997613822)
XLA Ops:
  0.0 81.6 %block_sparse.1 = bf16[1024,256]{1,0:T(8,128)(2,1)S(1)} custom-call(s32[65]{0:T(128)} %bitcast.10, s32[192]{0:T(256)} %bitcast.8, s32[1,65]{1,0:T(1,128)} %bitcast.11, s32[1,192]{1,0:T(1,128)} %bitcast.9, bf16[8,128,256]{2,1,0:T(8,128)(2,1)} %bitcast.7, bf16[192,128,128]{2,1,0:T(8,128)(2,1)} %bitcast.6), custom_call_target="tpu_custom_call" | custom-call | tf_op jit(solution)/shard_map/block_sparse/pallas_call | solution.py:433
  81.6 0.8 copy.6
